TPU v7x, 16 devices: a 4x2x1 block of a 4x4x8 slice. The times are simulated.
16 devices in a mesh: dp: 2 (over y, z), tp: 8 (over x, core).
Axes of the slice: x: 4, y: 2, z: 1, core: 2. Of those that a mesh axis runs over, the one named last changes fastest.
The devices are a block of a 4x4x8 slice.
Arguments:
- x_in: bfloat16 [256, 4096], P('dp'), parts along dimension 0
- seq_lens: int32 [256], P('dp'), parts along dimension 0
- g_attn: bfloat16 [2, 4096], replicated
- g_mlp: bfloat16 [2, 4096], replicated
- w_q: bfloat16 [2, 4096, 4096], P(None, None, 'tp')
- b_q: bfloat16 [2, 4096], P(None, 'tp')
- w_k: bfloat16 [2, 4096, 1024], P(None, None, 'tp')
- b_k: bfloat16 [2, 1024], P(None, 'tp')
- w_v: bfloat16 [2, 4096, 1024], P(None, None, 'tp')
- b_v: bfloat16 [2, 1024], P(None, 'tp')
- w_o: bfloat16 [2, 4096, 4096], P(None, 'tp')
- w_gate: bfloat16 [2, 4096, 12288], P(None, None, 'tp')
- w_up: bfloat16 [2, 4096, 12288], P(None, None, 'tp')
- w_down: bfloat16 [2, 12288, 4096], P(None, 'tp')
- k_cache: bfloat16 [2, 256, 128, 8, 128], P(None, 'dp', None, 'tp'), parts along dimension 1
- v_cache: bfloat16 [2, 256, 128, 8, 128], P(None, 'dp', None, 'tp'), parts along dimension 1
Outputs:
- output 1: bfloat16 [256, 4096], P('dp'), parts along dimension 0
- output 2: bfloat16 [2, 256, 128, 8, 128], P(None, 'dp', None, 'tp'), parts along dimension 1
- output 3: bfloat16 [2, 256, 128, 8, 128], P(None, 'dp', None, 'tp'), parts along dimension 1
There are 2 independent parts. A program takes and returns all parts, laid end to end along the dimension named above; an argument that names none is the same for every part.
All inputs are finite; a program needn't handle non-finite values.
Results may differ from a plain program's by a relative error of at most 0.02.
Values are sent between devices in bfloat16 or wider.
A program may use at most 768 MiB of HBM per device.

v0:
```python
import jax
import jax.numpy as jnp
from jax import lax
from jax.sharding import PartitionSpec as P

ROPE_THETA = 1000000.0
EPS = 1e-6


def rms_norm(vec_in, gain_vec):
    vec_f32 = vec_in.astype(jnp.float32)
    mean_sq = jnp.mean(vec_f32 * vec_f32, axis=-1, keepdims=True)
    return (vec_f32 * lax.rsqrt(mean_sq + EPS) * gain_vec.astype(jnp.float32)).astype(jnp.bfloat16)


def rope_tables(seq_lens, head_dim):
    half_dim = head_dim // 2
    inv_freq = ROPE_THETA ** (-2.0 * jnp.arange(half_dim, dtype=jnp.float32) / head_dim)
    angles = seq_lens.astype(jnp.float32)[:, None] * inv_freq[None, :]
    angles = jnp.concatenate([angles, angles], axis=-1)[:, None, :]
    return jnp.cos(angles), jnp.sin(angles)


def apply_rope(vec_in, cos_tab, sin_tab):
    half_dim = vec_in.shape[-1] // 2
    rotated = jnp.concatenate([-vec_in[..., half_dim:], vec_in[..., :half_dim]], axis=-1)
    return vec_in * cos_tab + rotated * sin_tab


def attention(normed, seq_lens, cos_tab, sin_tab, w_q, b_q, w_k, b_k, w_v, b_v, k_cache, v_cache):
    num_rows, num_slots, kv_local, head_dim = k_cache.shape
    q_local = w_q.shape[1] // head_dim
    group_size = q_local // kv_local
    q_full = jnp.dot(normed, w_q, preferred_element_type=jnp.float32) + b_q.astype(jnp.float32)
    q_rot = apply_rope(q_full.reshape(num_rows, q_local, head_dim), cos_tab, sin_tab).astype(jnp.bfloat16)
    k_full = jnp.dot(normed, w_k, preferred_element_type=jnp.float32) + b_k.astype(jnp.float32)
    k_rot = apply_rope(k_full.reshape(num_rows, kv_local, head_dim), cos_tab, sin_tab).astype(jnp.bfloat16)
    v_full = jnp.dot(normed, w_v, preferred_element_type=jnp.float32) + b_v.astype(jnp.float32)
    v_new = v_full.astype(jnp.bfloat16).reshape(num_rows, kv_local, head_dim)
    slot_ids = lax.broadcasted_iota(jnp.int32, (1, num_slots), 1)
    is_new = (slot_ids == seq_lens[:, None])[:, :, None, None]
    k_next = jnp.where(is_new, k_rot[:, None], k_cache)
    v_next = jnp.where(is_new, v_new[:, None], v_cache)
    q_grouped = q_rot.reshape(num_rows, kv_local, group_size, head_dim)
    scores = jnp.einsum("bkgd,bskd->bkgs", q_grouped, k_next, preferred_element_type=jnp.float32) * (head_dim ** -0.5)
    visible = (slot_ids <= seq_lens[:, None])[:, None, None, :]
    scores = jnp.where(visible, scores, -1e30)
    attn_probs = jax.nn.softmax(scores, axis=-1).astype(jnp.bfloat16)
    attn_out = jnp.einsum("bkgs,bskd->bkgd", attn_probs, v_next, preferred_element_type=jnp.float32)
    return attn_out.astype(jnp.bfloat16).reshape(num_rows, q_local * head_dim), k_next, v_next


def mlp_partial(normed, w_gate, w_up, w_down):
    gate_proj = jnp.dot(normed, w_gate, preferred_element_type=jnp.float32)
    up_proj = jnp.dot(normed, w_up, preferred_element_type=jnp.float32)
    hidden_act = (jax.nn.silu(gate_proj) * up_proj).astype(jnp.bfloat16)
    return jnp.dot(hidden_act, w_down, preferred_element_type=jnp.float32)


def add_residual(x_cur, delta):
    return (x_cur.astype(jnp.float32) + delta.astype(jnp.float32)).astype(jnp.bfloat16)


def solution(mesh):
    weight_col = P(None, None, "tp")
    weight_row = P(None, "tp", None)
    bias_col = P(None, "tp")
    cache_spec = P(None, "dp", None, "tp", None)
    in_specs = (P("dp", None), P("dp"), P(None, None), P(None, None), weight_col, bias_col, weight_col, bias_col, weight_col, bias_col, weight_row, weight_col, weight_col, weight_row, cache_spec, cache_spec)
    out_specs = (P("dp", None), cache_spec, cache_spec)

    def local_step(x_in, seq_lens, g_attn, g_mlp, w_q, b_q, w_k, b_k, w_v, b_v, w_o, w_gate, w_up, w_down, k_cache, v_cache):
        cos_tab, sin_tab = rope_tables(seq_lens, k_cache.shape[-1])
        x_cur = x_in
        k_list = []
        v_list = []
        for layer_idx in range(w_q.shape[0]):
            normed = rms_norm(x_cur, g_attn[layer_idx])
            attn_out, k_next, v_next = attention(normed, seq_lens, cos_tab, sin_tab, w_q[layer_idx], b_q[layer_idx], w_k[layer_idx], b_k[layer_idx], w_v[layer_idx], b_v[layer_idx], k_cache[layer_idx], v_cache[layer_idx])
            k_list.append(k_next)
            v_list.append(v_next)
            attn_part = jnp.dot(attn_out, w_o[layer_idx], preferred_element_type=jnp.float32).astype(jnp.bfloat16)
            x_cur = add_residual(x_cur, lax.psum(attn_part, "tp"))
            mlp_part = mlp_partial(rms_norm(x_cur, g_mlp[layer_idx]), w_gate[layer_idx], w_up[layer_idx], w_down[layer_idx]).astype(jnp.bfloat16)
            x_cur = add_residual(x_cur, lax.psum(mlp_part, "tp"))
        return x_cur, jnp.stack(k_list), jnp.stack(v_list)

    return jax.shard_map(local_step, mesh=mesh, in_specs=in_specs, out_specs=out_specs, check_vma=False)
```

profile of v0, /device:TPU:113, one launch (start us, length us, event | category | flops | bytes accessed | tf_op | source)
XLA Modules:
  0.0 324.7 jit_solution(587814495708789412)
XLA Ops:
  8.8 1.5 fusion.60
  10.3 1.3 bitcast_convert_fusion.1
  11.5 1.2 bitcast_convert_fusion
  12.8 1.3 slice_convert_fusion.4
  14.1 1.4 slice_convert_fusion.3
  15.5 2.2 convolution_add_fusion.3
  18.4 3.0 fusion.84
  21.7 1.7 fusion.94
  23.5 5.3 %fusion.151 = (f32[128,4]{1,0:T(8,128)S(1)}, f32[128,4,128]{2,1,0:T(4,128)S(1)}) fusion(pred[128,128]{1,0:T(8,128)(4,1)S(1)} %get-tuple-element.35, bf16[2,128,128,1,128]{4,2,1,3,0:T(8,128)(2,1)} %bitcast.138, bf16[128,128]{1,0:T(8,128)(2,1)S(1)} %copy.21, f32[128,4,64]{2,1,0:T(4,128)S(1)} %get-tuple-element.15, f32[128,4,64]{2,1,0:T(4,128)S(1)} %get-tuple-element.14, ...), kind=kOutput, calls=%fused_computation.177 | convolution fusion | flops 19464320 | bytes 5179392 | tf_op jit(solution)/shard_map/sub | solution.py:48
  28.8 4.8 %fusion.92 = bf16[128,4,128]{2,1,0:T(4,128)(2,1)S(1)} fusion(pred[128,128]{1,0:T(8,128)(4,1)S(1)} %get-tuple-element.35, bf16[2,128,128,1,128]{4,2,1,3,0:T(8,128)(2,1)} %bitcast.141, bf16[128,128]{1,0:T(8,128)(2,1)S(1)} %fusion.94, f32[128,4,128]{2,1,0:T(4,128)S(1)} %get-tuple-element.37, f32[128,4]{1,0:T(8,128)S(1)} %get-tuple-element.36), kind=kOutput, calls=%fused_computation.100 | convolution fusion | flops 19070976 | bytes 4638720 | tf_op jit(solution)/shard_map/bkgs,bskd->bkgd/dot_general | solution.py:49
  33.6 3.9 %convolution_convert_fusion.1 = bf16[128,4096]{1,0:T(8,128)(2,1)} fusion(bf16[2,512,4096]{2,1,0:T(8,128)(2,1)} %param.26, bf16[16,8,4,128]{3,2,1,0:T(4,128)(2,1)S(1)} %bitcast.155), kind=kOutput, calls=%fused_computation.26 | convolution fusion | flops 537395200 | bytes 5373952 | tf_op jit(solution)/shard_map/dot_general | solution.py:82
  38.3 54.7 %all-reduce.5.cloned.1.call-done = bf16[128,4096]{1,0:T(8,128)(2,1)} async-done(((bf16[128,4096]{1,0:T(8,128)(2,1)}), bf16[128,4096]{1,0:T(8,128)(2,1)}) %all-reduce.5.cloned.1.call-update) | async-done | bytes 1048592 | tf_op jit(solution)/shard_map/psum | solution.py:83
  93.0 1.7 fusion.64
  94.7 5.7 %fusion.12 = f32[128,1536]{1,0:T(8,128)S(1)} fusion(bf16[2,4096,1536]{2,1,0:T(8,128)(2,1)} %param.27, bf16[128,4096]{1,0:T(8,128)(2,1)S(1)} %get-tuple-element.9, f32[4096]{0:T(1024)S(1)} %bitcast.151, f32[128]{0:T(128)S(1)} %add_rsqrt_fusion.2), kind=kOutput, calls=%fused_computation.12 | convolution fusion | flops 1612709888 | bytes 14434816 | tf_op jit(solution)/shard_map/dot_general | solution.py:54
  100.3 11.8 %fusion.20 = bf16[128,4096]{1,0:T(8,128)(2,1)} fusion(bf16[2,1536,4096]{2,1,0:T(8,128)(2,1)} %param.29, bf16[2,4096,1536]{2,1,0:T(8,128)(2,1)} %param.28, f32[128,1536]{1,0:T(8,128)S(1)} %fusion.12, bf16[128,4096]{1,0:T(8,128)(2,1)S(1)} %get-tuple-element.9, f32[4096]{0:T(1024)S(1)} %bitcast.152, f32[128]{0:T(128)S(1)} %add_rsqrt_fusion.2), kind=kOutput, calls=%fused_computation.23 | convolution fusion | flops 3225026560 | bytes 28066304 | tf_op jit(solution)/shard_map/dot_general | solution.py:57
  112.5 53.5 %all-reduce.7.cloned.1.call-done = bf16[128,4096]{1,0:T(8,128)(2,1)} async-done(((bf16[128,4096]{1,0:T(8,128)(2,1)}), bf16[128,4096]{1,0:T(8,128)(2,1)}) %all-reduce.7.cloned.1.call-update) | async-done | bytes 1048592 | tf_op jit(solution)/shard_map/psum | solution.py:85
  166.0 1.8 fusion.68
  167.8 1.6 fusion.70
  171.1 2.9 fusion.87
  174.8 5.3 %fusion.152 = (f32[128,4]{1,0:T(8,128)S(1)}, f32[128,4,128]{2,1,0:T(4,128)S(1)}) fusion(pred[128,128]{1,0:T(8,128)(4,1)S(1)} %get-tuple-element.35, bf16[2,128,128,1,128]{4,2,1,3,0:T(8,128)(2,1)} %bitcast.139, bf16[128,128]{1,0:T(8,128)(2,1)S(1)} %copy.24, f32[128,4,64]{2,1,0:T(4,128)S(1)} %get-tuple-element.13, f32[128,4,64]{2,1,0:T(4,128)S(1)} %get-tuple-element.12, ...), kind=kOutput, calls=%fused_computation.178 | convolution fusion | flops 19464320 | bytes 5179392 | tf_op jit(solution)/shard_map/sub | solution.py:48
  180.1 4.8 %fusion.93 = bf16[128,4,128]{2,1,0:T(4,128)(2,1)S(1)} fusion(pred[128,128]{1,0:T(8,128)(4,1)S(1)} %get-tuple-element.35, bf16[2,128,128,1,128]{4,2,3,1,0:T(8,128)(2,1)} %param.31, bf16[128,128]{1,0:T(8,128)(2,1)S(1)} %copy-done.12, f32[128,4,128]{2,1,0:T(4,128)S(1)} %get-tuple-element.39, f32[128,4]{1,0:T(8,128)S(1)} %get-tuple-element.38), kind=kOutput, calls=%fused_computation.101 | convolution fusion | flops 19070976 | bytes 4638720 | tf_op jit(solution)/shard_map/bkgs,bskd->bkgd/dot_general | solution.py:49
  185.0 3.9 %convolution_convert_fusion = bf16[128,4096]{1,0:T(8,128)(2,1)} fusion(bf16[2,512,4096]{2,1,0:T(8,128)(2,1)} %param.26, bf16[16,8,4,128]{3,2,1,0:T(4,128)(2,1)S(1)} %bitcast.156), kind=kOutput, calls=%fused_computation.25 | convolution fusion | flops 537395200 | bytes 5373952 | tf_op jit(solution)/shard_map/dot_general | solution.py:82
  189.0 9.9 %broadcast_select_fusion.1 = (bf16[1,128,128,1,128]{4,2,1,3,0:T(8,128)(2,1)}, bf16[1,128,128,1,128]{4,2,1,3,0:T(8,128)(2,1)}, bf16[1,128,128,1,128]{4,2,3,1,0:T(8,128)(2,1)}) fusion(pred[128,128]{1,0:T(8,128)(4,1)S(1)} %get-tuple-element.35, bf16[2,128,128,1,128]{4,2,1,3,0:T(8,128)(2,1)} %bitcast.140, bf16[128,128]{1,0:T(8,128)(2,1)S(1)} %copy.21, ...), kind=kLoop, calls=%fused_computation.47 | loop fusion | flops 6291456 | bytes 25280512 | tf_op jit(solution)/shard_map/jit(_where)/select_n | solution.py:42
  198.9 7.8 %bitcast_select_fusion = bf16[1,128,128,1,128]{4,2,3,1,0:T(8,128)(2,1)} fusion(pred[128,128]{1,0:T(8,128)(4,1)S(1)} %get-tuple-element.35, bf16[2,128,128,1,128]{4,2,3,1,0:T(8,128)(2,1)} %param.31, bf16[128,128]{1,0:T(8,128)(2,1)S(1)} %copy-done.12), kind=kLoop, calls=%fused_computation.22 | loop fusion | flops 2097152 | bytes 8437760 | tf_op jit(solution)/shard_map/jit(_where)/select_n | solution.py:43
  206.6 36.0 %all-reduce.9.cloned.1.call-done = bf16[128,4096]{1,0:T(8,128)(2,1)} async-done(((bf16[128,4096]{1,0:T(8,128)(2,1)}), bf16[128,4096]{1,0:T(8,128)(2,1)}) %all-reduce.9.cloned.1.call-update) | async-done | bytes 1048592 | tf_op jit(solution)/shard_map/psum | solution.py:83
  242.6 1.8 fusion.72
  244.4 5.7 %fusion.6 = f32[128,1536]{1,0:T(8,128)S(1)} fusion(bf16[2,4096,1536]{2,1,0:T(8,128)(2,1)} %param.27, bf16[128,4096]{1,0:T(8,128)(2,1)S(1)} %get-tuple-element.7, f32[4096]{0:T(1024)S(1)} %bitcast.146, f32[128]{0:T(128)S(1)} %add_rsqrt_fusion), kind=kOutput, calls=%fused_computation.6 | convolution fusion | flops 1612709888 | bytes 14434816 | tf_op jit(solution)/shard_map/dot_general | solution.py:54
  250.1 11.8 %fusion.23 = bf16[128,4096]{1,0:T(8,128)(2,1)} fusion(bf16[2,1536,4096]{2,1,0:T(8,128)(2,1)} %param.29, bf16[2,4096,1536]{2,1,0:T(8,128)(2,1)} %param.28, f32[128,1536]{1,0:T(8,128)S(1)} %fusion.6, bf16[128,4096]{1,0:T(8,128)(2,1)S(1)} %get-tuple-element.7, f32[4096]{0:T(1024)S(1)} %bitcast.147, f32[128]{0:T(128)S(1)} %add_rsqrt_fusion), kind=kOutput, calls=%fused_computation.24 | convolution fusion | flops 3225026560 | bytes 28066304 | tf_op jit(solution)/shard_map/dot_general | solution.py:57
  262.0 7.8 %maximum_bitcast_fusion = bf16[2,128,128,1,128]{4,2,3,1,0:T(8,128)(2,1)} fusion(bf16[1,128,128,1,128]{4,2,1,3,0:T(8,128)(2,1)} %get-tuple-element.11, bf16[1,128,128,1,128]{4,2,1,3,0:T(8,128)(2,1)} %get-tuple-element.10), kind=kLoop, calls=%fused_computation.20 | loop fusion | flops 4194304 | bytes 16777216
  269.8 6.3 %pad_maximum_fusion = bf16[2,128,128,1,128]{4,2,3,1,0:T(8,128)(2,1)} fusion(bf16[1,128,128,1,128]{4,2,3,1,0:T(8,128)(2,1)S(1)} %copy-done, bf16[1,128,128,1,128]{4,2,3,1,0:T(8,128)(2,1)} %get-tuple-element.23), kind=kLoop, calls=%fused_computation.21 | loop fusion | flops 4194304 | bytes 16777216 | tf_op jit(solution)/shard_map/stack | solution.py:86
  276.1 39.6 %all-reduce.11.cloned.1.call-done = bf16[128,4096]{1,0:T(8,128)(2,1)} async-done(((bf16[128,4096]{1,0:T(8,128)(2,1)}), bf16[128,4096]{1,0:T(8,128)(2,1)}) %all-reduce.11.cloned.1.call-update) | async-done | bytes 1048592 | tf_op jit(solution)/shard_map/psum | solution.py:85
  315.7 2.4 fusion.75
  (71 shorter events, 6.0 us)
Async XLA Ops:
  7.2 11.2 %copy-start.2 = (bf16[128,4096]{1,0:T(8,128)(2,1)S(1)}, bf16[128,4096]{1,0:T(8,128)(2,1)}, u32[]{:S(2)}) copy-start(bf16[128,4096]{1,0:T(8,128)(2,1)} %param.16) | copy-start | bytes 3145732
  7.2 85.8 %all-reduce.5.cloned.1.call-start = ((), (), s32[]{:S(2)}) async-start(), calls=%async_computation | async-start | bytes 2097152 | tf_op jit(solution)/shard_map/psum | solution.py:83
  8.7 14.7 %copy-start.13 = (pred[128,128]{1,0:T(8,128)(4,1)}, pred[128,128]{1,0:T(8,128)(4,1)S(1)}, u32[]{:S(2)}) copy-start(pred[128,128]{1,0:T(8,128)(4,1)S(1)} %get-tuple-element.34) | copy-start | bytes 49156
  18.2 5.3 %copy-start.5 = (f32[128,128]{1,0:T(8,128)}, f32[128,128]{1,0:T(8,128)S(1)}, u32[]{:S(2)}) copy-start(f32[128,128]{1,0:T(8,128)S(1)} %copy.19) | copy-start | bytes 196612
  18.4 5.1 %copy-start.7 = (f32[128,128]{1,0:T(8,128)}, f32[128,128]{1,0:T(8,128)S(1)}, u32[]{:S(2)}) copy-start(f32[128,128]{1,0:T(8,128)S(1)} %copy.20) | copy-start | bytes 196612
  23.4 5.4 %copy-start.10 = (bf16[128,128]{1,0:T(8,128)(2,1)}, bf16[128,128]{1,0:T(8,128)(2,1)S(1)}, u32[]{:S(2)}) copy-start(bf16[128,128]{1,0:T(8,128)(2,1)S(1)} %fusion.94) | copy-start | bytes 98308
  33.6 4.0 %copy-start.9 = (bf16[2,4096]{1,0:T(2,128)(2,1)S(1)}, bf16[2,4096]{1,0:T(2,128)(2,1)}, u32[]{:S(2)}) copy-start(bf16[2,4096]{1,0:T(2,128)(2,1)} %param.19) | copy-start | bytes 49156
  37.6 128.4 %all-reduce.7.cloned.1.call-start = ((), (), s32[]{:S(2)}) async-start(), calls=%async_computation.1 | async-start | bytes 2097152 | tf_op jit(solution)/shard_map/psum | solution.py:85
  100.3 67.5 %copy-start.4 = (f32[1,4096]{1,0:T(1,128)S(1)}, f32[1,4096]{1,0:T(1,128)}, u32[]{:S(2)}) copy-start(f32[1,4096]{1,0:T(1,128)} %get-tuple-element.27) | copy-start | bytes 49156
  112.1 57.3 %copy-start.18 = (f32[128]{0:T(128)S(1)}, f32[128]{0:T(128)}, u32[]{:S(2)}) copy-start(f32[128]{0:T(128)} %get-tuple-element.32) | copy-start | bytes 1540
  112.1 58.4 %copy-start.3 = (bf16[2,4096,128]{2,1,0:T(8,128)(2,1)S(1)}, bf16[2,4096,128]{2,1,0:T(8,128)(2,1)}, u32[]{:S(2)}) copy-start(bf16[2,4096,128]{2,1,0:T(8,128)(2,1)} %param.22) | copy-start | bytes 6291460
  112.2 58.4 %copy-start.16 = (f32[128]{0:T(128)S(1)}, f32[128]{0:T(128)}, u32[]{:S(2)}) copy-start(f32[128]{0:T(128)} %get-tuple-element.30) | copy-start | bytes 1540
  112.2 130.4 %all-reduce.9.cloned.1.call-start = ((), (), s32[]{:S(2)}) async-start(), calls=%async_computation.2 | async-start | bytes 2097152 | tf_op jit(solution)/shard_map/psum | solution.py:83
  166.0 3.5 %copy-start.19 = (bf16[2,4096,128]{2,1,0:T(8,128)(2,1)S(1)}, bf16[2,4096,128]{2,1,0:T(8,128)(2,1)}, u32[]{:S(2)}) copy-start(bf16[2,4096,128]{2,1,0:T(8,128)(2,1)} %param.24) | copy-start | bytes 6291460
  167.8 3.3 %copy-start.17 = (f32[1,512]{1,0:T(1,128)S(1)}, f32[1,512]{1,0:T(1,128)}, u32[]{:S(2)}) copy-start(f32[1,512]{1,0:T(1,128)} %get-tuple-element.28) | copy-start | bytes 6148
  171.1 3.7 %copy-start.6 = (f32[128,128]{1,0:T(8,128)S(1)}, f32[128,128]{1,0:T(8,128)}, u32[]{:S(2)}) copy-start(f32[128,128]{1,0:T(8,128)} %copy-done.5) | copy-start | bytes 196612
  171.1 3.7 %copy-start.8 = (f32[128,128]{1,0:T(8,128)S(1)}, f32[128,128]{1,0:T(8,128)}, u32[]{:S(2)}) copy-start(f32[128,128]{1,0:T(8,128)} %copy-done.7) | copy-start | bytes 196612
  171.1 3.7 %copy-start.14 = (pred[128,128]{1,0:T(8,128)(4,1)S(1)}, pred[128,128]{1,0:T(8,128)(4,1)}, u32[]{:S(2)}) copy-start(pred[128,128]{1,0:T(8,128)(4,1)} %copy-done.13) | copy-start | bytes 49156
  174.8 5.3 %copy-start.12 = (bf16[128,128]{1,0:T(8,128)(2,1)S(1)}, bf16[128,128]{1,0:T(8,128)(2,1)}, u32[]{:S(2)}) copy-start(bf16[128,128]{1,0:T(8,128)(2,1)} %fusion.95) | copy-start | bytes 98308
  185.0 4.0 %copy-start.11 = (bf16[128,128]{1,0:T(8,128)(2,1)S(1)}, bf16[128,128]{1,0:T(8,128)(2,1)}, u32[]{:S(2)}) copy-start(bf16[128,128]{1,0:T(8,128)(2,1)} %copy-done.10) | copy-start | bytes 98308
  188.9 126.8 %all-reduce.11.cloned.1.call-start = ((), (), s32[]{:S(2)}) async-start(), calls=%async_computation.3 | async-start | bytes 2097152 | tf_op jit(solution)/shard_map/psum | solution.py:85
  198.9 43.7 %copy-start.1 = (bf16[128,4096]{1,0:T(8,128)(2,1)S(1)}, bf16[128,4096]{1,0:T(8,128)(2,1)}, u32[]{:S(2)}) copy-start(bf16[128,4096]{1,0:T(8,128)(2,1)} %all-reduce.7.cloned.1.call-done) | copy-start | bytes 3145732
  206.6 37.8 %copy-start.15 = (f32[1,4096]{1,0:T(1,128)S(1)}, f32[1,4096]{1,0:T(1,128)}, u32[]{:S(2)}) copy-start(f32[1,4096]{1,0:T(1,128)} %get-tuple-element.24) | copy-start | bytes 49156
  262.0 7.8 %copy-start = (bf16[1,128,128,1,128]{4,2,3,1,0:T(8,128)(2,1)S(1)}, bf16[1,128,128,1,128]{4,2,3,1,0:T(8,128)(2,1)}, u32[]{:S(2)}) copy-start(bf16[1,128,128,1,128]{4,2,3,1,0:T(8,128)(2,1)} %bitcast_select_fusion) | copy-start | bytes 12582916
Sparse Core Ops, SparseCore 0:
  37.7 55.2 all-reduce.4
  112.3 53.6 all-reduce.6
  189.0 53.5 all-reduce.8
  262.1 53.5 all-reduce.10
where the time goes:
time: 328 us; the launch traced here: 325 us
  waiting for transfers between devices  184 us (56%)
  matrix products  74.4 us (23%)
  other arithmetic  51 us (16%)
  between operations  14.2 us (4%)
    psum x2, waiting for transfers between devices, local_step(): x_cur = add_residual(x_cur, lax.psum(mlp_part, 'tp'))  93.1 us
    psum x2, waiting for transfers between devices, local_step(): x_cur = add_residual(x_cur, lax.psum(attn_part, 'tp'))  90.6 us
    dot_general x2, matrix products, mlp_partial(): return jnp.dot(hidden_act, w_down, preferred_element_type=jnp.float32)  23.6 us
    dot_general x2, matrix products, mlp_partial(): gate_proj = jnp.dot(normed, w_gate, preferred_element_type=jnp.float32)  11.4 us
    sub x2, matrix products, attention(): attn_probs = jax.nn.softmax(scores, axis=-1).astype(jnp.bfloat16)  10.6 us
    select_n x1, other arithmetic, attention(): k_next = jnp.where(is_new, k_rot[:, None], k_cache)  9.89 us
    dot_general x2, matrix products, attention(): jnp.einsum('bkgs,bskd->bkgd', attn_probs, v_next, preferred_element_type=...  9.64 us
    dot_general x2, matrix products, local_step(): jnp.dot(attn_out, w_o[layer_idx], preferred_element_type=jnp.float32)  7.79 us
  transfers between devices with their start and end apart: 4, of which 4 were waited for; matrix products, arithmetic and copies ran while one was open for 10% of the time, Pallas kernels for 0%

commit v1 on v0

v1 whole, which is shorter than its diff:
```python
import functools
import math

import jax
import jax.numpy as jnp
from jax import lax
from jax.experimental import pallas as pl
from jax.experimental.pallas import tpu as pltpu
from jax.sharding import PartitionSpec as P

ROPE_THETA = 1000000.0
EPS = 1e-6
MESH = pl.DeviceIdType.MESH
BF16 = jnp.bfloat16
F32 = jnp.float32
NCHUNK = 4
SEQ_BLOCK = 16
HBM = pl.BlockSpec(memory_space=pltpu.HBM)
VMEM = pl.BlockSpec(memory_space=pltpu.VMEM)
SMEM = pl.BlockSpec(memory_space=pltpu.SMEM)


def attention_kernel(layer, first, seq_ref, act_ref, g_ref, bq_ref, bk_ref, bv_ref, cos_in, sin_in, wq, wk, wv, kc, vc,
                     *rest):
    rest = list(rest)
    if not first:
        rest = rest[2:]
    attn_ref, cos_ref, sin_ref, k_out, v_out = rest[:5]
    h_s, w_s, kbuf, vbuf, qs, os, kn, vn, wsem, csem, osem = rest[5:]
    rows, width = act_ref.shape
    q_width = wq.shape[2]
    head = wk.shape[2]
    slots = kbuf.shape[1]
    heads = q_width // head
    kw = width // NCHUNK
    nblk = rows // SEQ_BLOCK

    def w_copies(c):
        ks = pl.ds(c * kw, kw)
        return [
            pltpu.make_async_copy(wq.at[layer, ks, :], w_s.at[ks, pl.ds(0, q_width)], wsem.at[c, 0]),
            pltpu.make_async_copy(wk.at[layer, ks, :], w_s.at[ks, pl.ds(q_width, head)], wsem.at[c, 1]),
            pltpu.make_async_copy(wv.at[layer, ks, :], w_s.at[ks, pl.ds(q_width + head, head)], wsem.at[c, 2]),
        ]

    def c_copies(i):
        bs = pl.ds(i * SEQ_BLOCK, SEQ_BLOCK)
        return [
            pltpu.make_async_copy(kc.at[layer, bs], kbuf.at[bs], csem.at[i, 0]),
            pltpu.make_async_copy(vc.at[layer, bs], vbuf.at[bs], csem.at[i, 1]),
        ]

    def o_copies(i):
        bs = pl.ds(i * SEQ_BLOCK, SEQ_BLOCK)
        return [
            pltpu.make_async_copy(kbuf.at[bs], k_out.at[layer, bs], osem.at[i, 0]),
            pltpu.make_async_copy(vbuf.at[bs], v_out.at[layer, bs], osem.at[i, 1]),
        ]

    for c in range(NCHUNK):
        for cp in w_copies(c):
            cp.start()
    for i in range(nblk):
        for cp in c_copies(i):
            cp.start()

    if first:
        def pos_row(b, carry):
            kn[pl.ds(b, 1), :] = jnp.full((1, head), seq_ref[b].astype(F32))
            return carry
        lax.fori_loop(0, rows, pos_row, 0, unroll=8)
        lane = lax.broadcasted_iota(jnp.int32, (rows, head), 1)
        half = head // 2
        freq = (lane % half).astype(F32)
        inv_freq = jnp.exp(freq[:8] * (-2.0 / head * math.log(ROPE_THETA)))
        angle = kn[...] * jnp.broadcast_to(inv_freq[:1], (rows, head))
        cos_ref[...] = jnp.cos(angle)
        sin_ref[...] = jnp.where(lane < half, -1.0, 1.0) * jnp.sin(angle)

        def norm_block(i, carry):
            rs = pl.ds(pl.multiple_of(i * 16, 16), 16)
            xv = act_ref[rs, :].astype(F32)
            ms = jnp.mean(xv * xv, axis=-1, keepdims=True)
            gain = g_ref[...].astype(F32)[layer:layer + 1, :]
            h_s[rs, :] = (xv * lax.rsqrt(ms + EPS) * gain).astype(BF16)
            return carry
        lax.fori_loop(0, rows // 16, norm_block, 0)
        h_src = h_s
    else:
        cos_ref[...] = cos_in[...]
        sin_ref[...] = sin_in[...]
        h_src = act_ref

    acc = None
    for c in range(NCHUNK):
        for cp in w_copies(c):
            cp.wait()
        part = jnp.dot(h_src[:, c * kw:(c + 1) * kw], w_s[c * kw:(c + 1) * kw, :], preferred_element_type=F32)
        acc = part if acc is None else acc + part
    cos_t = cos_ref[...]
    sin_t = sin_ref[...]

    def rope(vec):
        return vec * cos_t + pltpu.roll(vec, head // 2, 1) * sin_t

    bq = bq_ref[...].astype(F32)[layer:layer + 1, :]
    bk = bk_ref[...].astype(F32)[layer:layer + 1, :]
    bv = bv_ref[...].astype(F32)[layer:layer + 1, :]
    for j in range(heads):
        cols = slice(j * head, (j + 1) * head)
        qs[pl.ds(j, rows, stride=8), :] = rope(acc[:, cols] + bq[:, cols])
    kn[...] = rope(acc[:, q_width:q_width + head] + bk)
    vn[...] = acc[:, q_width + head:] + bv

    scale = head ** -0.5

    def block(i, carry):
        b0 = i * SEQ_BLOCK
        for cp in c_copies(i):
            cp.wait()
        slot = lax.broadcasted_iota(jnp.int32, (slots, head), 0)
        lane = lax.broadcasted_iota(jnp.int32, (8, slots), 1)
        for j in range(SEQ_BLOCK):
            b = b0 + j
            pos = seq_ref[b]
            is_new = slot == pos
            k_b = jnp.where(is_new, jnp.broadcast_to(kn[pl.ds(b, 1), :], (slots, head)), kbuf[b].astype(F32)).astype(BF16)
            v_b = jnp.where(is_new, jnp.broadcast_to(vn[pl.ds(b, 1), :], (slots, head)), vbuf[b].astype(F32)).astype(BF16)
            kbuf[b] = k_b
            vbuf[b] = v_b
            q_b = qs[pl.ds(pl.multiple_of(b * 8, 8), 8), :].astype(BF16)
            sc = lax.dot_general(q_b, k_b, (((1,), (1,)), ((), ())), preferred_element_type=F32) * scale
            sc = jnp.where(lane <= pos, sc, -1e30)
            e = jnp.exp(sc - jnp.max(sc, axis=-1, keepdims=True))
            pr = (e / jnp.sum(e, axis=-1, keepdims=True)).astype(BF16)
            os[pl.ds(pl.multiple_of(b * 8, 8), 8), :] = jnp.dot(pr, v_b, preferred_element_type=F32)
        for cp in o_copies(i):
            cp.start()
        return carry

    lax.fori_loop(0, nblk, block, 0)
    for j in range(heads):
        attn_ref[:, j * head:(j + 1) * head] = os[pl.ds(j, rows, stride=8), :].astype(BF16)
    for i in range(nblk):
        for cp in o_copies(i):
            cp.wait()


def attention_call(layer, seq_lens, act, g_attn, b_q, b_k, b_v, cos_t, sin_t, w_q, w_k, w_v, kc, vc, outs):
    first = outs is None
    rows, width = act.shape
    head = w_k.shape[2]
    q_width = w_q.shape[2]
    slots = kc.shape[2]
    nblk = rows // SEQ_BLOCK
    table = jax.ShapeDtypeStruct((rows, head), F32)
    operands = [seq_lens, act, g_attn, b_q, b_k, b_v, cos_t, sin_t, w_q, w_k, w_v, kc, vc]
    in_specs = [SMEM, VMEM, VMEM, VMEM, VMEM, VMEM, VMEM, VMEM, HBM, HBM, HBM, HBM, HBM]
    aliases = {}
    if not first:
        aliases = {len(operands): 3, len(operands) + 1: 4}
        operands += list(outs)
        in_specs += [HBM, HBM]
    return pl.pallas_call(
        functools.partial(attention_kernel, layer, first),
        out_shape=(jax.ShapeDtypeStruct((rows, q_width), BF16), table, table,
                   jax.ShapeDtypeStruct(kc.shape, BF16), jax.ShapeDtypeStruct(vc.shape, BF16)),
        in_specs=in_specs,
        out_specs=(VMEM, VMEM, VMEM, HBM, HBM),
        scratch_shapes=[
            pltpu.VMEM((rows, width), BF16),
            pltpu.VMEM((width, q_width + 2 * head), BF16),
            pltpu.VMEM((rows, slots, head), BF16),
            pltpu.VMEM((rows, slots, head), BF16),
            pltpu.VMEM((rows * 8, head), F32),
            pltpu.VMEM((rows * 8, head), F32),
            pltpu.VMEM((rows, head), F32),
            pltpu.VMEM((rows, head), F32),
            pltpu.SemaphoreType.DMA((NCHUNK, 3)),
            pltpu.SemaphoreType.DMA((nblk, 2)),
            pltpu.SemaphoreType.DMA((nblk, 2)),
        ],
        input_output_aliases=aliases,
        compiler_params=pltpu.CompilerParams(vmem_limit_bytes=62 << 20),
        name=f"attention_{layer}",
    )(*operands)


def mlp_kernel(layer, last, attn_ref, x_ref, gm_ref, gn_ref, wo, wg, wu, wd, *rest):
    n_out = 1 if last else 2
    outs = rest[:n_out]
    (wo_s, wg_s, wu_s, wd_s, part, r0, sa, sk, r1, sb, r2, xs, hbuf, gacc, uacc, act,
     wsem, xsem, ssem, rsem) = rest[n_out:]
    rows, width = hbuf.shape[1:]
    cw = width // NCHUNK
    unit = rows // 8
    me = lax.axis_index("tp")
    core = me % 2
    chip = me // 2
    flip_near = chip + 1 - 2 * (chip % 2)
    flip_far = 3 - chip
    bit_near = ((chip + 1) // 2) % 2
    bit_far = chip // 2
    dev_p = chip * 2 + 1 - core
    dev_a = ((1 - core) * flip_near + core * flip_far) * 2 + core
    dev_b = ((1 - core) * flip_far + core * flip_near) * 2 + core
    bit_a = (1 - core) * bit_near + core * bit_far
    bit_b = (1 - core) * bit_far + core * bit_near

    def row0(core_, a_, b_):
        return pl.multiple_of((core_ * 4 + a_ * 2 + b_) * unit, unit)

    own = row0(core, bit_a, bit_b)

    def wo_copy(c):
        return pltpu.make_async_copy(wo.at[layer, :, pl.ds(c * cw, cw)], wo_s.at[:, pl.ds(c * cw, cw)], wsem.at[0, c])

    def wg_copy(c):
        return pltpu.make_async_copy(wg.at[layer, pl.ds(c * cw, cw), :], wg_s.at[pl.ds(c * cw, cw), :], wsem.at[1, c])

    def wu_copy(c):
        return pltpu.make_async_copy(wu.at[layer, pl.ds(c * cw, cw), :], wu_s.at[pl.ds(c * cw, cw), :], wsem.at[2, c])

    def wd_copy(c):
        return pltpu.make_async_copy(wd.at[layer, :, pl.ds(c * cw, cw)], wd_s.at[:, pl.ds(c * cw, cw)], wsem.at[3, c])

    for c in range(NCHUNK):
        wo_copy(c).start()
    x_copy = None
    if x_ref.shape[0] != unit:
        x_copy = pltpu.make_async_copy(x_ref.at[pl.ds(own, unit), :], xs, xsem)
        x_copy.start()
    else:
        xs[...] = x_ref[...]

    barrier = pltpu.get_barrier_semaphore()
    for dev in (dev_p, dev_a, dev_b):
        pl.semaphore_signal(barrier, inc=1, device_id={"tp": dev}, device_id_type=MESH)
    pl.semaphore_wait(barrier, 3)

    def rcopy(ar, c, k, src, dst, dev):
        return pltpu.make_async_remote_copy(
            src_ref=src, dst_ref=dst, send_sem=ssem.at[ar, c, k], recv_sem=rsem.at[ar, c, k],
            device_id={"tp": dev}, device_id_type=MESH)

    def rs_p(ar, c):
        src = part.at[ar, c, pl.ds(pl.multiple_of((1 - core) * 4 * unit, unit), 4 * unit), :]
        return rcopy(ar, c, 0, src, r0.at[ar, c], dev_p)

    def rs_a(ar, c, k):
        return rcopy(ar, c, 1 + k, sa.at[ar, c, k], r1.at[ar, c, k], dev_a)

    def rs_b(ar, c):
        return rcopy(ar, c, 3, sb.at[ar, c], r2.at[ar, c], dev_b)

    def ag(ar, c, k, start, dev):
        blk = hbuf.at[ar, pl.ds(start, unit), pl.ds(c * cw, cw)]
        return rcopy(ar, c, 4 + k, blk, blk, dev)

    blk_b = row0(core, bit_a, 1 - bit_b)
    blk_a0 = row0(core, 1 - bit_a, bit_b)
    blk_a1 = row0(core, 1 - bit_a, 1 - bit_b)

    def ag_b(ar, c):
        return ag(ar, c, 0, own, dev_b)

    def ag_a(ar, c, k):
        return ag(ar, c, 1 + k, (own, blk_b)[k], dev_a)

    def ag_p(ar, c, k):
        return ag(ar, c, 3 + k, (own, blk_b, blk_a0, blk_a1)[k], dev_p)

    def reduce_scatter(ar, make_part):
        for c in range(NCHUNK):
            part[ar, c] = make_part(c).astype(BF16)
            rs_p(ar, c).start()
        for c in range(NCHUNK):
            rs_p(ar, c).wait_recv()

            def chip_sum(a_, b_):
                mine = part[ar, c, pl.ds(row0(core, a_, b_), unit), :].astype(F32)
                theirs = r0[ar, c, pl.ds(row0(0, a_, b_), unit), :].astype(F32)
                return mine + theirs

            sa[ar, c, 0] = chip_sum(1 - bit_a, 1 - bit_b).astype(BF16)
            rs_a(ar, c, 0).start()
            sa[ar, c, 1] = chip_sum(1 - bit_a, bit_b).astype(BF16)
            sk[c, 0] = chip_sum(bit_a, 1 - bit_b)
            sk[c, 1] = chip_sum(bit_a, bit_b)
        for c in range(NCHUNK):
            rs_a(ar, c, 1).start()
        for c in range(NCHUNK):
            rs_a(ar, c, 0).wait_recv()
            sb[ar, c] = (sk[c, 0] + r1[ar, c, 0].astype(F32)).astype(BF16)
            rs_b(ar, c).start()
        for c in range(NCHUNK):
            rs_a(ar, c, 1).wait_recv()
            rs_b(ar, c).wait_recv()
            delta = sk[c, 1] + r1[ar, c, 1].astype(F32) + r2[ar, c].astype(F32)
            cols = slice(c * cw, (c + 1) * cw)
            xs[:, cols] = (xs[:, cols].astype(F32) + delta).astype(BF16)

    def gather_start(ar):
        for c in range(NCHUNK):
            ag_b(ar, c).start()
            ag_a(ar, c, 0).start()
            ag_p(ar, c, 0).start()
        for c in range(NCHUNK):
            ag_b(ar, c).wait_recv()
            ag_a(ar, c, 1).start()
            ag_p(ar, c, 1).start()
        for c in range(NCHUNK):
            ag_a(ar, c, 0).wait_recv()
            ag_p(ar, c, 2).start()
        for c in range(NCHUNK):
            ag_a(ar, c, 1).wait_recv()
            ag_p(ar, c, 3).start()

    def gather_wait(ar, c):
        for k in range(4):
            ag_p(ar, c, k).wait_recv()

    def norm_own(gain):
        xv = xs[...].astype(F32)
        ms = jnp.mean(xv * xv, axis=-1, keepdims=True)
        return (xv * lax.rsqrt(ms + EPS) * gain).astype(BF16)

    def wo_part(c):
        wo_copy(c).wait()
        if c == NCHUNK - 1:
            for i in range(NCHUNK):
                wg_copy(i).start()
                wu_copy(i).start()
            for i in range(NCHUNK):
                wd_copy(i).start()
        return jnp.dot(attn_ref[...], wo_s[:, c * cw:(c + 1) * cw], preferred_element_type=F32)

    if x_copy is not None:
        x_copy.wait()
    reduce_scatter(0, wo_part)
    hbuf[0, pl.ds(own, unit), :] = norm_own(gm_ref[...].astype(F32)[layer:layer + 1, :])
    gather_start(0)
    for c in range(NCHUNK):
        gather_wait(0, c)
        wg_copy(c).wait()
        wu_copy(c).wait()
        ks = slice(c * cw, (c + 1) * cw)
        hc = hbuf[0, :, ks]
        gp = jnp.dot(hc, wg_s[ks, :], preferred_element_type=F32)
        up = jnp.dot(hc, wu_s[ks, :], preferred_element_type=F32)
        if c == 0:
            gacc[...] = gp
            uacc[...] = up
        elif c < NCHUNK - 1:
            gacc[...] += gp
            uacc[...] += up
        else:
            gate = gacc[...] + gp
            act[...] = (gate * jax.nn.sigmoid(gate) * (uacc[...] + up)).astype(BF16)

    def wd_part(c):
        wd_copy(c).wait()
        return jnp.dot(act[...], wd_s[:, c * cw:(c + 1) * cw], preferred_element_type=F32)

    reduce_scatter(1, wd_part)
    if last:
        hbuf[1, pl.ds(own, unit), :] = xs[...]
    else:
        hbuf[1, pl.ds(own, unit), :] = norm_own(gn_ref[...].astype(F32)[layer + 1:layer + 2, :])
        outs[1][...] = xs[...]
    gather_start(1)
    for c in range(NCHUNK):
        gather_wait(1, c)
        outs[0][:, c * cw:(c + 1) * cw] = hbuf[1, :, c * cw:(c + 1) * cw]
    for ar in range(2):
        for c in range(NCHUNK):
            rs_p(ar, c).wait_send()
            rs_b(ar, c).wait_send()
            ag_b(ar, c).wait_send()
            for k in range(2):
                rs_a(ar, c, k).wait_send()
                ag_a(ar, c, k).wait_send()
            for k in range(4):
                ag_p(ar, c, k).wait_send()


def mlp_call(layer, last, attn, x_res, g_mlp, g_attn, w_o, w_gate, w_up, w_down):
    rows = attn.shape[0]
    width = w_o.shape[2]
    inner = w_o.shape[1]
    ff = w_gate.shape[2]
    unit = rows // 8
    cw = width // NCHUNK
    full = jax.ShapeDtypeStruct((rows, width), BF16)
    out_shape = (full,) if last else (full, jax.ShapeDtypeStruct((unit, width), BF16))
    x_spec = VMEM if x_res.shape[0] == unit else HBM
    return pl.pallas_call(
        functools.partial(mlp_kernel, layer, last),
        out_shape=out_shape,
        in_specs=[VMEM, x_spec, VMEM, VMEM, HBM, HBM, HBM, HBM],
        out_specs=(VMEM,) * len(out_shape),
        scratch_shapes=[
            pltpu.VMEM((inner, width), BF16),
            pltpu.VMEM((width, ff), BF16),
            pltpu.VMEM((width, ff), BF16),
            pltpu.VMEM((ff, width), BF16),
            pltpu.VMEM((2, NCHUNK, rows, cw), BF16),
            pltpu.VMEM((2, NCHUNK, rows // 2, cw), BF16),
            pltpu.VMEM((2, NCHUNK, 2, unit, cw), BF16),
            pltpu.VMEM((NCHUNK, 2, unit, cw), F32),
            pltpu.VMEM((2, NCHUNK, 2, unit, cw), BF16),
            pltpu.VMEM((2, NCHUNK, unit, cw), BF16),
            pltpu.VMEM((2, NCHUNK, unit, cw), BF16),
            pltpu.VMEM((unit, width), BF16),
            pltpu.VMEM((2, rows, width), BF16),
            pltpu.VMEM((rows, ff), F32),
            pltpu.VMEM((rows, ff), F32),
            pltpu.VMEM((rows, ff), BF16),
            pltpu.SemaphoreType.DMA((4, NCHUNK)),
            pltpu.SemaphoreType.DMA,
            pltpu.SemaphoreType.DMA((2, NCHUNK, 11)),
            pltpu.SemaphoreType.DMA((2, NCHUNK, 11)),
        ],
        compiler_params=pltpu.CompilerParams(
            vmem_limit_bytes=62 << 20, collective_id=layer, has_side_effects=True),
        name=f"mlp_{layer}",
    )(attn, x_res, g_mlp, g_attn, w_o, w_gate, w_up, w_down)


def solution(mesh):
    assert mesh.shape["tp"] == 8
    weight_col = P(None, None, "tp")
    weight_row = P(None, "tp", None)
    bias_col = P(None, "tp")
    cache_spec = P(None, "dp", None, "tp", None)
    in_specs = (P("dp", None), P("dp"), P(None, None), P(None, None), weight_col, bias_col, weight_col, bias_col, weight_col, bias_col, weight_row, weight_col, weight_col, weight_row, cache_spec, cache_spec)
    out_specs = (P("dp", None), cache_spec, cache_spec)

    def local_step(x_in, seq_lens, g_attn, g_mlp, w_q, b_q, w_k, b_k, w_v, b_v, w_o, w_gate, w_up, w_down, k_cache, v_cache):
        num_layers, rows, slots, kv_local, head = k_cache.shape
        kc = k_cache.reshape(num_layers, rows, slots, kv_local * head)
        vc = v_cache.reshape(num_layers, rows, slots, kv_local * head)
        act, x_res, outs = x_in, x_in, None
        cos_t = sin_t = jnp.zeros((8, head), F32)
        for layer in range(num_layers):
            last = layer == num_layers - 1
            attn, cos_t, sin_t, *outs = attention_call(
                layer, seq_lens, act, g_attn, b_q, b_k, b_v, cos_t, sin_t, w_q, w_k, w_v, kc, vc, outs)
            res = mlp_call(layer, last, attn, x_res, g_mlp, g_attn, w_o, w_gate, w_up, w_down)
            if last:
                x_out = res[0]
            else:
                act, x_res = res
        return x_out, outs[0].reshape(k_cache.shape), outs[1].reshape(v_cache.shape)

    return jax.shard_map(local_step, mesh=mesh, in_specs=in_specs, out_specs=out_specs, check_vma=False)
```

time: 328 us -> 197 us (0.60)
  Pallas kernels: 0 us -> 193 us
  waiting for transfers between devices: 184 us -> 0 us
  matrix products: 74.4 us -> 0 us
  other arithmetic: 51 us -> 0 us
  between operations: 14.2 us -> 0.66 us
    pallas_call x0 -> x4, Pallas kernels: none -> 193 us  [the longest x2 99.3 us: attention_call(): pl.pallas_call(functools.partial(attention_kernel, layer, first), out_sha...]
    psum x4 -> x0, waiting for transfers between devices: 184 us -> none  [the longest x2 93.1 us: local_step(): x_cur = add_residual(x_cur, lax.psum(mlp_part, 'tp'))]
    dot_general x14 -> x0, matrix products: 63.8 us -> none  [the longest x2 23.6 us: mlp_partial(): return jnp.dot(hidden_act, w_down, preferred_element_type=jnp.float32)]
    select_n x2 -> x0, other arithmetic: 17.6 us -> none  [the longest x1 9.89 us: attention(): k_next = jnp.where(is_new, k_rot[:, None], k_cache)]
    sub x2 -> x0, matrix products: 10.6 us -> none  [attention(): attn_probs = jax.nn.softmax(scores, axis=-1).astype(jnp.bfloat16)]
    unnamed x1 -> x0, other arithmetic: 7.76 us -> none
    reduce_sum x4 -> x0, other arithmetic: 6.8 us -> none  [rms_norm(): mean_sq = jnp.mean(vec_f32 * vec_f32, axis=-1, keepdims=True)]
    another operation x1 -> x0, other arithmetic: 6.35 us -> none  [local_step(): return (x_cur, jnp.stack(k_list), jnp.stack(v_list))]
  transfers between devices with their start and end apart: 4 -> 0, of which waited for: 4 -> 0; matrix products, arithmetic and copies ran while one was open for 10% -> 0% of each run, Pallas kernels for 0% -> 0%
where the time goes in v1:
time: 197 us; the launch traced here: 196 us
  Pallas kernels  193 us (98%)
  local copies, waits for them, and re-layouts  2.88 us (1%)
    pallas_call x2, Pallas kernels, attention_call(): pl.pallas_call(functools.partial(attention_kernel, layer, first), out_sha...  99.3 us
    pallas_call x2, Pallas kernels, mlp_call(): pl.pallas_call(functools.partial(mlp_kernel, layer, last), out_shape=out_...  93.3 us

profile of v1, /device:TPU:113, one launch (start us, length us, event | category | flops | bytes accessed | tf_op | source)
XLA Modules:
  0.0 196.1 jit_solution(10727339291234858463)
XLA Ops:
  0.6 0.6 broadcast_in_dim.3.cos_in.sin_in
  1.2 49.6 %attention_0.1 = (bf16[128,512]{1,0:T(8,128)(2,1)}, f32[128,128]{1,0:T(8,128)}, f32[128,128]{1,0:T(8,128)}, bf16[2,128,128,128]{3,2,1,0:T(8,128)(2,1)}, bf16[2,128,128,128]{3,2,1,0:T(8,128)(2,1)}) custom-call(s32[128]{0:T(128)} %seq_ref.3, bf16[128,4096]{1,0:T(8,128)(2,1)} %x_ref.1, bf16[2,4096]{1,0:T(2,128)(2,1)} %gn_ref.3, bf16[2,512]{1,0:T(2,128)(2,1)} %bq_ref.3, ...), custom_call_target="tpu_custom_call" | custom-call | tf_op jit(solution)/shard_map/attention_0/pallas_call | solution.py:164
  50.8 46.8 %mlp_0.1 = (bf16[128,4096]{1,0:T(8,128)(2,1)}, bf16[16,4096]{1,0:T(8,128)(2,1)}) custom-call(bf16[128,512]{1,0:T(8,128)(2,1)} %get-tuple-element.13.attn_ref, bf16[128,4096]{1,0:T(8,128)(2,1)} %x_ref.1, bf16[2,4096]{1,0:T(2,128)(2,1)} %gm_ref.3, bf16[2,4096]{1,0:T(2,128)(2,1)} %gn_ref.3, bf16[2,512,4096]{2,1,0:T(8,128)(2,1)} %wo.3, ...), custom_call_target="tpu_custom_call" | custom-call | tf_op jit(solution)/shard_map/mlp_0/pallas_call | solution.py:397
  97.7 49.8 %attention_1.1 = (bf16[128,512]{1,0:T(8,128)(2,1)}, f32[128,128]{1,0:T(8,128)}, f32[128,128]{1,0:T(8,128)}, bf16[2,128,128,128]{3,2,1,0:T(8,128)(2,1)}, bf16[2,128,128,128]{3,2,1,0:T(8,128)(2,1)}) custom-call(s32[128]{0:T(128)} %seq_ref.3, bf16[128,4096]{1,0:T(8,128)(2,1)} %get-tuple-element.14.act_ref, ...), custom_call_target="tpu_custom_call", output_to_operand_aliasing={{3}: (13, {}), {4}: (14, {})} | custom-call | tf_op jit(solution)/shard_map/attention_1/pallas_call | solution.py:164
  147.4 46.4 %mlp_1.1 = bf16[128,4096]{1,0:T(8,128)(2,1)} custom-call(bf16[128,512]{1,0:T(8,128)(2,1)} %get-tuple-element.19.attn_ref, bf16[16,4096]{1,0:T(8,128)(2,1)} %get-tuple-element.20.x_ref, bf16[2,4096]{1,0:T(2,128)(2,1)} %gm_ref.3, bf16[2,4096]{1,0:T(2,128)(2,1)} %gn_ref.3, bf16[2,512,4096]{2,1,0:T(8,128)(2,1)} %wo.3, bf16[2,4096,1536]{2,1,0:T(8,128)(2,1)} %wg.3, ...), custom_call_target="tpu_custom_call" | custom-call | tf_op jit(solution)/shard_map/mlp_1/pallas_call | solution.py:397
  193.9 2.3 %copy.26 = bf16[128,4096]{1,0:T(8,128)(2,1)} copy(bf16[128,4096]{1,0:T(8,128)(2,1)} %mlp_1.1) | data formatting | bytes 2097152

commit v2 on v1

--- a/solution.py
+++ b/solution.py
@@ -118,24 +118,36 @@
         b0 = i * SEQ_BLOCK
         for cp in c_copies(i):
             cp.wait()
-        slot = lax.broadcasted_iota(jnp.int32, (slots, head), 0)
+        tile_row = lax.broadcasted_iota(jnp.int32, (16, head), 0)
         lane = lax.broadcasted_iota(jnp.int32, (8, slots), 1)
         for j in range(SEQ_BLOCK):
             b = b0 + j
             pos = seq_ref[b]
-            is_new = slot == pos
-            k_b = jnp.where(is_new, jnp.broadcast_to(kn[pl.ds(b, 1), :], (slots, head)), kbuf[b].astype(F32)).astype(BF16)
-            v_b = jnp.where(is_new, jnp.broadcast_to(vn[pl.ds(b, 1), :], (slots, head)), vbuf[b].astype(F32)).astype(BF16)
-            kbuf[b] = k_b
-            vbuf[b] = v_b
-            q_b = qs[pl.ds(pl.multiple_of(b * 8, 8), 8), :].astype(BF16)
-            sc = lax.dot_general(q_b, k_b, (((1,), (1,)), ((), ())), preferred_element_type=F32) * scale
-            sc = jnp.where(lane <= pos, sc, -1e30)
-            e = jnp.exp(sc - jnp.max(sc, axis=-1, keepdims=True))
-            pr = (e / jnp.sum(e, axis=-1, keepdims=True)).astype(BF16)
-            os[pl.ds(pl.multiple_of(b * 8, 8), 8), :] = jnp.dot(pr, v_b, preferred_element_type=F32)
+            base = pl.multiple_of((pos // 16) * 16, 16)
+            is_new = tile_row == pos - base
+            for buf, new in ((kbuf, kn), (vbuf, vn)):
+                old = buf[b, pl.ds(base, 16), :].astype(F32)
+                row = jnp.broadcast_to(new[pl.ds(b, 1), :], (16, head))
+                buf[b, pl.ds(base, 16), :] = jnp.where(is_new, row, old).astype(BF16)
         for cp in o_copies(i):
             cp.start()
+        scores = []
+        for j in range(0, SEQ_BLOCK, 2):
+            b = b0 + j
+            q_pair = qs[pl.ds(pl.multiple_of(b * 8, 16), 16), :].astype(BF16)
+            k_pair = kbuf[pl.ds(b, 2)].reshape(2 * slots, head)
+            sc = lax.dot_general(q_pair, k_pair, (((1,), (1,)), ((), ())), preferred_element_type=F32) * scale
+            scores.append(jnp.where(lane <= seq_ref[b], sc[:8, :slots], -1e30))
+            scores.append(jnp.where(lane <= seq_ref[b + 1], sc[8:, slots:], -1e30))
+        sc = jnp.concatenate(scores, axis=0)
+        e = jnp.exp(sc - jnp.max(sc, axis=-1, keepdims=True))
+        pr = (e / jnp.sum(e, axis=-1, keepdims=True)).astype(BF16)
+        for j in range(0, SEQ_BLOCK, 2):
+            b = b0 + j
+            v_pair = jnp.concatenate([vbuf[b], vbuf[b + 1]], axis=1)
+            o_pair = jnp.dot(pr[j * 8:j * 8 + 16, :], v_pair, preferred_element_type=F32)
+            os[pl.ds(pl.multiple_of(b * 8, 16), 8), :] = o_pair[:8, :head]
+            os[pl.ds(pl.multiple_of(b * 8, 16) + 8, 8), :] = o_pair[8:, head:]
         return carry
 
     lax.fori_loop(0, nblk, block, 0)

time: 197 us -> 125 us (0.63)
  Pallas kernels: 193 us -> 121 us
    pallas_call x2, Pallas kernels: 99.3 us -> 27.4 us  [attention_call(): pl.pallas_call(functools.partial(attention_kernel, layer, first), out_sha...]
where the time goes in v2:
time: 125 us; the launch traced here: 124 us
  Pallas kernels  121 us (97%)
  local copies, waits for them, and re-layouts  2.88 us (2%)
    pallas_call x2, Pallas kernels, mlp_call(): pl.pallas_call(functools.partial(mlp_kernel, layer, last), out_shape=out_...  93.2 us
    pallas_call x2, Pallas kernels, attention_call(): pl.pallas_call(functools.partial(attention_kernel, layer, first), out_sha...  27.4 us

profile of v2, /device:TPU:113, one launch (start us, length us, event | category | flops | bytes accessed | tf_op | source)
XLA Modules:
  0.0 124.1 jit_solution(2617470168000691490)
XLA Ops:
  0.6 0.6 broadcast_in_dim.3.cos_in.sin_in
  1.2 13.7 %attention_0.1 = (bf16[128,512]{1,0:T(8,128)(2,1)}, f32[128,128]{1,0:T(8,128)}, f32[128,128]{1,0:T(8,128)}, bf16[2,128,128,128]{3,2,1,0:T(8,128)(2,1)}, bf16[2,128,128,128]{3,2,1,0:T(8,128)(2,1)}) custom-call(s32[128]{0:T(128)} %seq_ref.3, bf16[128,4096]{1,0:T(8,128)(2,1)} %x_ref.1, bf16[2,4096]{1,0:T(2,128)(2,1)} %gn_ref.3, bf16[2,512]{1,0:T(2,128)(2,1)} %bq_ref.3, ...), custom_call_target="tpu_custom_call" | custom-call | tf_op jit(solution)/shard_map/attention_0/pallas_call | solution.py:176
  14.9 46.8 %mlp_0.1 = (bf16[128,4096]{1,0:T(8,128)(2,1)}, bf16[16,4096]{1,0:T(8,128)(2,1)}) custom-call(bf16[128,512]{1,0:T(8,128)(2,1)} %get-tuple-element.13.attn_ref, bf16[128,4096]{1,0:T(8,128)(2,1)} %x_ref.1, bf16[2,4096]{1,0:T(2,128)(2,1)} %gm_ref.3, bf16[2,4096]{1,0:T(2,128)(2,1)} %gn_ref.3, bf16[2,512,4096]{2,1,0:T(8,128)(2,1)} %wo.3, ...), custom_call_target="tpu_custom_call" | custom-call | tf_op jit(solution)/shard_map/mlp_0/pallas_call | solution.py:409
  61.8 13.7 %attention_1.1 = (bf16[128,512]{1,0:T(8,128)(2,1)}, f32[128,128]{1,0:T(8,128)}, f32[128,128]{1,0:T(8,128)}, bf16[2,128,128,128]{3,2,1,0:T(8,128)(2,1)}, bf16[2,128,128,128]{3,2,1,0:T(8,128)(2,1)}) custom-call(s32[128]{0:T(128)} %seq_ref.3, bf16[128,4096]{1,0:T(8,128)(2,1)} %get-tuple-element.14.act_ref, ...), custom_call_target="tpu_custom_call", output_to_operand_aliasing={{3}: (13, {}), {4}: (14, {})} | custom-call | tf_op jit(solution)/shard_map/attention_1/pallas_call | solution.py:176
  75.5 46.4 %mlp_1.1 = bf16[128,4096]{1,0:T(8,128)(2,1)} custom-call(bf16[128,512]{1,0:T(8,128)(2,1)} %get-tuple-element.19.attn_ref, bf16[16,4096]{1,0:T(8,128)(2,1)} %get-tuple-element.20.x_ref, bf16[2,4096]{1,0:T(2,128)(2,1)} %gm_ref.3, bf16[2,4096]{1,0:T(2,128)(2,1)} %gn_ref.3, bf16[2,512,4096]{2,1,0:T(8,128)(2,1)} %wo.3, bf16[2,4096,1536]{2,1,0:T(8,128)(2,1)} %wg.3, ...), custom_call_target="tpu_custom_call" | custom-call | tf_op jit(solution)/shard_map/mlp_1/pallas_call | solution.py:409
  121.8 2.3 %copy.26 = bf16[128,4096]{1,0:T(8,128)(2,1)} copy(bf16[128,4096]{1,0:T(8,128)(2,1)} %mlp_1.1) | data formatting | bytes 2097152
